TPU v7x, 32 devices: a whole 2x2x4 slice. The times are simulated.
32 devices in a mesh: seq: 16 (over z, y, x), rep: 2 (over core).
Axes of the slice: x: 2, y: 2, z: 4, core: 2. Of those that a mesh axis runs over, the one named last changes fastest.
Arguments:
- tokens: bfloat16 [4, 48, 180, 768], P('rep', 'seq'), may hold values from -6 to 6
- cotangent: bfloat16 [4, 48, 180, 768], P('rep', 'seq'), may hold values from -6 to 6
- in_weight: bfloat16 [2, 8, 96, 96], replicated, may hold values from -0.21875 to 0.21875
- in_bias: float32 [2, 768], replicated, may hold values from -0.6 to 0.6
- out_weight: bfloat16 [2, 8, 96, 96], replicated, may hold values from -0.21875 to 0.21875
- out_bias: float32 [2, 768], replicated, may hold values from -0.12 to 0.12
Outputs:
- mixed_out: bfloat16 [4, 48, 180, 768], P('rep', 'seq')
- tokens_grad: bfloat16 [4, 48, 180, 768], P('rep', 'seq')
- in_weight_grad: float32 [2, 8, 96, 96], replicated
- in_bias_grad: float32 [2, 768], replicated
- out_weight_grad: float32 [2, 8, 96, 96], replicated
- out_bias_grad: float32 [2, 768], replicated
All inputs are finite; a program needn't handle non-finite values.
Results may differ from a plain program's by a relative error of at most 0.0094.
Values may be sent and summed in bfloat16 or wider, within the bound.
A program may use at most 64 MiB of HBM per device.

v0:
```python
import math

import jax
import jax.numpy as jnp
from jax import lax
from jax.sharding import PartitionSpec as P

BLOCKS = 8
BLOCK = 96
MODES = 64


def grid_tables(length, modes):
    position = jnp.arange(length, dtype=jnp.int32)
    frequency = jnp.arange(modes, dtype=jnp.int32)
    residue = position[:, None] * frequency[None, :] % length
    angles = residue.astype(jnp.float32) * (2.0 * math.pi / length)
    factor = 1.0 / math.sqrt(length)
    cosine_table = (jnp.cos(angles) * factor).astype(jnp.bfloat16)
    sine_table = (jnp.sin(angles) * factor).astype(jnp.bfloat16)
    return (cosine_table, sine_table)


def column_tables(grid_width, modes):
    cosine_table, sine_table = grid_tables(grid_width, modes)
    forward = jnp.stack([cosine_table, -sine_table], axis=2)
    doubling = jnp.where(jnp.arange(modes) == 0, 1.0, 2.0).astype(jnp.bfloat16)[:, None]
    inverse = jnp.stack([cosine_table.T * doubling, -(sine_table.T * doubling)], axis=1)
    return (forward, inverse)


def row_table(length):
    cosine_table, sine_table = grid_tables(length, length)
    upper_rows = jnp.stack([cosine_table, sine_table], axis=2)
    lower_rows = jnp.stack([-sine_table, cosine_table], axis=2)
    return jnp.stack([upper_rows, lower_rows], axis=1)


def block_weights(weight):
    real_part, imag_part = (weight[0], weight[1])
    upper_half = jnp.stack([real_part, imag_part], axis=2)
    lower_half = jnp.stack([-imag_part, real_part], axis=2)
    return jnp.stack([upper_half, lower_half], axis=1)


def fold_blocks(blockwise):
    real_part = blockwise[:, 0, :, 0, :] + blockwise[:, 1, :, 1, :]
    imag_part = blockwise[:, 0, :, 1, :] - blockwise[:, 1, :, 0, :]
    return jnp.stack([real_part, imag_part])


def mix_forward(spectrum, weights_in, weights_out, bias_in, bias_out):
    mode_count = spectrum.shape[0] * spectrum.shape[1] * spectrum.shape[2]
    flat_modes = spectrum.reshape(mode_count, 2, BLOCKS, BLOCK)
    hidden_pre = (
        jnp.einsum("mcbi,bciej->mebj", flat_modes, weights_in, preferred_element_type=jnp.float32)
        + bias_in
    )
    hidden = jax.nn.gelu(hidden_pre).astype(jnp.bfloat16)
    spectrum_out = (
        jnp.einsum("mcbi,bciej->mebj", hidden, weights_out, preferred_element_type=jnp.float32)
        + bias_out
    )
    return (
        flat_modes,
        hidden_pre,
        hidden,
        spectrum_out.astype(jnp.bfloat16).reshape(spectrum.shape),
    )


def mix_backward(flat_modes, hidden_pre, hidden, incoming, weights_in, weights_out):
    incoming_flat = incoming.reshape(flat_modes.shape)
    out_bias_part = jnp.sum(incoming_flat.astype(jnp.float32), axis=0).reshape(2, -1)
    out_weight_part = fold_blocks(
        jnp.einsum("mcbi,mebj->bciej", hidden, incoming_flat, preferred_element_type=jnp.float32)
    )
    hidden_grad = jnp.einsum(
        "mebj,bciej->mcbi", incoming_flat, weights_out, preferred_element_type=jnp.float32
    )
    pre_grad = jax.vjp(jax.nn.gelu, hidden_pre)[1](hidden_grad)[0].astype(jnp.bfloat16)
    in_bias_part = jnp.sum(pre_grad.astype(jnp.float32), axis=0).reshape(2, -1)
    in_weight_part = fold_blocks(
        jnp.einsum("mcbi,mebj->bciej", flat_modes, pre_grad, preferred_element_type=jnp.float32)
    )
    spectrum_grad = jnp.einsum(
        "mebj,bciej->mcbi", pre_grad, weights_in, preferred_element_type=jnp.float32
    )
    spectrum_grad = spectrum_grad.astype(jnp.bfloat16).reshape(incoming.shape)
    return (spectrum_grad, (in_weight_part, in_bias_part, out_weight_part, out_bias_part))


def shards(tokens, cotangent, in_weight, in_bias, out_weight, out_bias):
    samples, row_count, grid_width, channels = tokens.shape
    length = row_count * lax.axis_size("seq")
    column_forward, column_inverse = column_tables(grid_width, MODES)
    row_matrix = row_table(length)
    weights_in = block_weights(in_weight)
    weights_out = block_weights(out_weight)
    bias_in = in_bias.reshape(2, BLOCKS, BLOCK)
    bias_out = out_bias.reshape(2, BLOCKS, BLOCK)

    def along_rows(section):
        return jnp.einsum(
            "qehc,shkcd->sqked", row_matrix, section, preferred_element_type=jnp.float32
        ).astype(jnp.bfloat16)

    def back_rows(section):
        return jnp.einsum(
            "qehc,sqked->shkcd", row_matrix, section, preferred_element_type=jnp.float32
        ).astype(jnp.bfloat16)

    spec_rows = jnp.einsum(
        "shwd,wkc->shkcd", tokens, column_forward, preferred_element_type=jnp.float32
    ).astype(jnp.bfloat16)
    spectrum = along_rows(lax.all_to_all(spec_rows, "seq", split_axis=2, concat_axis=1, tiled=True))
    flat_modes, hidden_pre, hidden, spectrum_out = mix_forward(
        spectrum, weights_in, weights_out, bias_in, bias_out
    )
    mixed_grid = jnp.einsum(
        "shkcd,kcw->shwd",
        lax.all_to_all(back_rows(spectrum_out), "seq", split_axis=1, concat_axis=2, tiled=True),
        column_inverse,
        preferred_element_type=jnp.float32,
    )
    cot_rows = jnp.einsum(
        "shwd,kcw->shkcd", cotangent, column_inverse, preferred_element_type=jnp.float32
    ).astype(jnp.bfloat16)
    incoming = along_rows(lax.all_to_all(cot_rows, "seq", split_axis=2, concat_axis=1, tiled=True))
    spectrum_grad, partials = mix_backward(
        flat_modes, hidden_pre, hidden, incoming, weights_in, weights_out
    )
    adjoint_part = jnp.einsum(
        "shkcd,wkc->shwd",
        lax.all_to_all(back_rows(spectrum_grad), "seq", split_axis=1, concat_axis=2, tiled=True),
        column_forward,
        preferred_element_type=jnp.float32,
    )
    mixed_out = (tokens.astype(jnp.float32) + mixed_grid).astype(jnp.bfloat16)
    tokens_grad = (cotangent.astype(jnp.float32) + adjoint_part).astype(jnp.bfloat16)
    totals = lax.psum((partials[0], partials[1], partials[2], partials[3]), ("seq", "rep"))
    divisor = float(samples * lax.axis_size("rep"))
    return (
        mixed_out,
        tokens_grad,
        totals[0] / divisor,
        totals[1] / divisor,
        totals[2] / divisor,
        totals[3] / divisor,
    )


def solution(mesh):
    in_specs = (P("rep", "seq", None, None), P("rep", "seq", None, None), P(), P(), P(), P())
    out_specs = (P("rep", "seq", None, None), P("rep", "seq", None, None), P(), P(), P(), P())
    return jax.shard_map(shards, mesh=mesh, in_specs=in_specs, out_specs=out_specs, check_vma=False)
```

profile of v0, /device:TPU:7, one launch (start us, length us, event | category | flops | bytes accessed | tf_op | source)
XLA Modules:
  0.0 314.4 jit_solution(5726129648743128858)
XLA Ops:
  11.9 6.8 %all-to-all-start = ((bf16[2,3,64,2,768]{4,3,1,0,2:T(2,128)(2,1)}), bf16[2,3,64,2,768]{4,3,1,0,2:T(2,128)(2,1)S(1)}, u32[]{:S(2)}, u32[]{:S(2)}) async-start(bf16[2,3,64,2,768]{4,3,1,0,2:T(2,128)(2,1)} %copy.183), calls=%async_computation | async-start | bytes 2359296 | tf_op jit(solution)/shard_map/all_to_all | solution.py:116
  21.8 21.8 %all-to-all-done = bf16[2,3,64,2,768]{4,3,1,0,2:T(2,128)(2,1)S(1)} async-done(((bf16[2,3,64,2,768]{4,3,1,0,2:T(2,128)(2,1)}), bf16[2,3,64,2,768]{4,3,1,0,2:T(2,128)(2,1)S(1)}, u32[]{:S(2)}, u32[]{:S(2)}) %all-to-all-start) | async-done | bytes 1179680 | tf_op jit(solution)/shard_map/all_to_all | solution.py:116
  43.6 7.1 %all-to-all-start.2 = ((bf16[2,3,64,2,768]{4,3,1,0,2:T(2,128)(2,1)}), bf16[2,3,64,2,768]{4,3,1,0,2:T(2,128)(2,1)}, u32[]{:S(2)}, u32[]{:S(2)}) async-start(bf16[2,3,64,2,768]{4,3,1,0,2:T(2,128)(2,1)} %copy.198), calls=%async_computation.2 | async-start | bytes 2359296 | tf_op jit(solution)/shard_map/all_to_all | solution.py:129
  63.2 3.7 %reshape.381 = bf16[384,2,8,96]{3,2,1,0:T(8,128)(2,1)S(1)} reshape(bf16[2,48,4,2,768]{4,3,2,1,0:T(2,128)(2,1)} %copy.186) | data formatting | bytes 2359296 | tf_op jit(solution)/shard_map/reshape | solution.py:54
  66.8 8.5 %all-to-all-done.2 = bf16[2,3,64,2,768]{4,3,1,0,2:T(2,128)(2,1)} async-done(((bf16[2,3,64,2,768]{4,3,1,0,2:T(2,128)(2,1)}), bf16[2,3,64,2,768]{4,3,1,0,2:T(2,128)(2,1)}, u32[]{:S(2)}, u32[]{:S(2)}) %all-to-all-start.2) | async-done | bytes 1179680 | tf_op jit(solution)/shard_map/all_to_all | solution.py:129
  79.9 4.6 %reshape.383 = bf16[384,2,8,96]{3,2,1,0:T(8,128)(2,1)} reshape(bf16[2,48,4,2,768]{4,3,2,1,0:T(2,128)(2,1)} %copy.201) | data formatting | bytes 2359296 | tf_op jit(solution)/shard_map/reshape | solution.py:73
  86.5 3.0 convert_reduce_fusion.1
  92.3 2.9 copy.205
  95.2 4.7 %reshape.384 = bf16[2,48,4,2,768]{4,3,2,1,0:T(2,128)(2,1)} reshape(bf16[384,2,8,96]{3,2,1,0:T(8,128)(2,1)} %copy.205) | data formatting | bytes 2359296 | tf_op jit(solution)/shard_map/reshape | solution.py:89
  103.6 8.7 %all-to-all-start.3 = ((bf16[2,48,4,2,768]{4,3,2,0,1:T(2,128)(2,1)}), bf16[2,48,4,2,768]{4,3,2,0,1:T(2,128)(2,1)}, u32[]{:S(2)}, u32[]{:S(2)}) async-start(bf16[2,48,4,2,768]{4,3,2,0,1:T(2,128)(2,1)} %copy.208), calls=%async_computation.3 | async-start | bytes 2359296 | tf_op jit(solution)/shard_map/all_to_all | solution.py:135
  112.4 4.5 %fusion.12 = bf16[384,2,8,96]{0,3,1,2:T(8,128)(2,1)} fusion(f32[2,8,96]{2,0,1:T(2,128)S(1)} %copy.189, bf16[8,1,96,2,96]{2,4,1,3,0:T(8,128)(2,1)} %get-tuple-element.49, bf16[8,1,96,2,96]{2,4,1,3,0:T(8,128)(2,1)} %get-tuple-element.48, f32[8,2,96,384,1]{3,2,4,1,0:T(8,128)} %copy-done.6, f32[2,8,96]{2,0,1:T(2,128)S(1)} %copy.188), kind=kOutput, calls=%fused_computation.20 | convolution fusion | flops 233865216 | bytes 4141056 | tf_op jit(solution)/shard_map/mcbi,bciej->mebj/dot_general | solution.py:61
  116.9 2.9 copy.190
  119.7 4.6 %reshape.382 = bf16[2,48,4,2,768]{4,3,2,1,0:T(2,128)(2,1)} reshape(bf16[384,2,8,96]{3,2,1,0:T(8,128)(2,1)} %copy.190) | data formatting | bytes 2359296 | tf_op jit(solution)/shard_map/reshape | solution.py:68
  130.0 7.6 %all-to-all-done.3 = bf16[2,48,4,2,768]{4,3,2,0,1:T(2,128)(2,1)} async-done(((bf16[2,48,4,2,768]{4,3,2,0,1:T(2,128)(2,1)}), bf16[2,48,4,2,768]{4,3,2,0,1:T(2,128)(2,1)}, u32[]{:S(2)}, u32[]{:S(2)}) %all-to-all-start.3) | async-done | bytes 1179680 | tf_op jit(solution)/shard_map/all_to_all | solution.py:135
  137.7 6.8 %all-to-all-start.1 = ((bf16[2,48,4,2,768]{4,3,2,0,1:T(2,128)(2,1)}), bf16[2,48,4,2,768]{4,3,2,0,1:T(2,128)(2,1)}, u32[]{:S(2)}, u32[]{:S(2)}) async-start(bf16[2,48,4,2,768]{4,3,2,0,1:T(2,128)(2,1)} %copy.193), calls=%async_computation.1 | async-start | bytes 2359296 | tf_op jit(solution)/shard_map/all_to_all | solution.py:122
  144.5 2.8 fusion.18
  148.4 49.6 %all-reduce = (f32[2,768]{1,0:T(2,128)S(1)}, f32[2,768]{1,0:T(2,128)S(1)}) all-reduce(f32[2,768]{1,0:T(2,128)S(1)} %reshape.385, f32[2,768]{1,0:T(2,128)S(1)} %get-tuple-element.56), channel_id=1, replica_groups=mesh['seq'=16,'rep'=2] {'seq','rep'}, use_global_device_ids=true, to_apply=%region_2.3 | all-reduce | flops 3072 | bytes 24576 | tf_op jit(solution)/shard_map/psum | solution.py:141
  199.2 88.5 %all-reduce.4.cloned.1.call-done = (f32[2,8,96,96]{3,2,1,0:T(8,128)}, f32[2,8,96,96]{3,2,1,0:T(8,128)}) async-done(((f32[2,8,96,96]{3,2,1,0:T(8,128)}, f32[2,8,96,96]{3,2,1,0:T(8,128)}), (f32[2,8,96,96]{3,2,1,0:T(8,128)}, f32[2,8,96,96]{3,2,1,0:T(8,128)})) %all-reduce.4.cloned.1.call-update) | async-done | bytes 1179664 | tf_op jit(solution)/shard_map/psum | solution.py:141
  290.8 2.8 copy.210
  293.6 2.4 all_to_all.67
  296.7 2.5 copy.221
  299.1 2.8 copy.195
  302.0 2.5 all_to_all.59
  305.1 2.5 copy.220
  (92 shorter events, 45.6 us)
Async XLA Ops:
  7.4 2.2 copy-start.13
  7.7 2.0 copy-start.15
  11.9 7.1 %copy-start = (bf16[2,3,180,768]{3,0,2,1:T(2,128)(2,1)S(1)}, bf16[2,3,180,768]{3,0,2,1:T(2,128)(2,1)}, u32[]{:S(2)}) copy-start(bf16[2,3,180,768]{3,0,2,1:T(2,128)(2,1)} %param.7) | copy-start | bytes 4976644
  11.9 31.7 %all-to-all-start = ((bf16[2,3,64,2,768]{4,3,1,0,2:T(2,128)(2,1)}), bf16[2,3,64,2,768]{4,3,1,0,2:T(2,128)(2,1)S(1)}, u32[]{:S(2)}, u32[]{:S(2)}) async-start(bf16[2,3,64,2,768]{4,3,1,0,2:T(2,128)(2,1)} %copy.183), calls=%async_computation | async-start | bytes 2359296 | tf_op jit(solution)/shard_map/all_to_all | solution.py:116
  43.6 31.7 %all-to-all-start.2 = ((bf16[2,3,64,2,768]{4,3,1,0,2:T(2,128)(2,1)}), bf16[2,3,64,2,768]{4,3,1,0,2:T(2,128)(2,1)}, u32[]{:S(2)}, u32[]{:S(2)}) async-start(bf16[2,3,64,2,768]{4,3,1,0,2:T(2,128)(2,1)} %copy.198), calls=%async_computation.2 | async-start | bytes 2359296 | tf_op jit(solution)/shard_map/all_to_all | solution.py:129
  50.7 5.6 %copy-start.17 = (f32[2,768]{1,0:T(2,128)S(1)}, f32[2,768]{1,0:T(2,128)}, u32[]{:S(2)}) copy-start(f32[2,768]{1,0:T(2,128)} %param.9) | copy-start | bytes 18436
  56.3 2.5 copy-start.10
  84.5 2.0 copy-start.7
  84.5 2.0 copy-start.11
  84.5 2.0 copy-start.12
  86.5 3.1 copy-start.6
  86.5 4.1 %copy-start.4 = (bf16[8,1,96,2,96]{2,4,1,3,0:T(8,128)(2,1)S(1)}, bf16[8,1,96,2,96]{2,4,1,3,0:T(8,128)(2,1)}, u32[]{:S(2)}) copy-start(bf16[8,1,96,2,96]{2,4,1,3,0:T(8,128)(2,1)} %get-tuple-element.46) | copy-start | bytes 884740
  86.5 4.1 %copy-start.5 = (bf16[8,1,96,2,96]{2,4,1,3,0:T(8,128)(2,1)S(1)}, bf16[8,1,96,2,96]{2,4,1,3,0:T(8,128)(2,1)}, u32[]{:S(2)}) copy-start(bf16[8,1,96,2,96]{2,4,1,3,0:T(8,128)(2,1)} %get-tuple-element.47) | copy-start | bytes 884740
  89.6 1.0 copy-start.2
  103.6 8.7 %copy-start.18 = (f32[2,768]{1,0:T(2,128)S(1)}, f32[2,768]{1,0:T(2,128)}, u32[]{:S(2)}) copy-start(f32[2,768]{1,0:T(2,128)} %param.11) | copy-start | bytes 18436
  103.6 34.1 %all-to-all-start.3 = ((bf16[2,48,4,2,768]{4,3,2,0,1:T(2,128)(2,1)}), bf16[2,48,4,2,768]{4,3,2,0,1:T(2,128)(2,1)}, u32[]{:S(2)}, u32[]{:S(2)}) async-start(bf16[2,48,4,2,768]{4,3,2,0,1:T(2,128)(2,1)} %copy.208), calls=%async_computation.3 | async-start | bytes 2359296 | tf_op jit(solution)/shard_map/all_to_all | solution.py:135
  126.2 2.0 copy-start.3
  129.1 15.5 %copy-start.8 = (bf16[384,2,8,96]{3,2,1,0:T(8,128)(2,1)S(1)}, bf16[384,2,8,96]{3,2,1,0:T(8,128)(2,1)}, u32[]{:S(2)}) copy-start(bf16[384,2,8,96]{3,2,1,0:T(8,128)(2,1)} %reshape.383) | copy-start | bytes 3538948
  137.7 161.5 %all-to-all-start.1 = ((bf16[2,48,4,2,768]{4,3,2,0,1:T(2,128)(2,1)}), bf16[2,48,4,2,768]{4,3,2,0,1:T(2,128)(2,1)}, u32[]{:S(2)}, u32[]{:S(2)}) async-start(bf16[2,48,4,2,768]{4,3,2,0,1:T(2,128)(2,1)} %copy.193), calls=%async_computation.1 | async-start | bytes 2359296 | tf_op jit(solution)/shard_map/all_to_all | solution.py:122
  144.5 143.3 %all-reduce.4.cloned.1.call-start = ((), (), s32[]{:S(2)}) async-start(), calls=%async_computation.4 | async-start | bytes 3145728 | tf_op jit(solution)/shard_map/psum | solution.py:141
  287.7 2.2 copy-start.9
  293.6 2.4 copy-start.14
  293.6 2.4 copy-start.16
  302.0 2.5 copy-start.1
Sparse Core Ops, SparseCore 0:
  151.3 136.3 all-reduce.3
where the time goes:
time: 319 us; the launch traced here: 314 us
  waiting for transfers between devices  126 us (39%)
  local copies, waits for them, and re-layouts  60.8 us (19%)
  blocking collectives  49.6 us (16%)
  starting transfers between devices  29.5 us (9%)
  matrix products  23.1 us (7%)
  between operations  14.4 us (5%)
  other arithmetic  10.7 us (3%)
    psum x1, waiting for transfers between devices, shards(): lax.psum((partials[0], partials[1], partials[2], partials[3]), ('seq', 'r...  88.5 us
    psum x1, blocking collectives, shards(): lax.psum((partials[0], partials[1], partials[2], partials[3]), ('seq', 'r...  49.6 us
    all_to_all x1, waiting for transfers between devices, shards(): lax.all_to_all(spec_rows, 'seq', split_axis=2, concat_axis=1, tiled=True)  21.8 us
    unnamed x44, local copies, waits for them, and re-layouts  8.82 us
    all_to_all x1, starting transfers between devices, shards(): lax.all_to_all(back_rows(spectrum_grad), 'seq', split_axis=1, concat_axis...  8.72 us
    all_to_all x1, waiting for transfers between devices, shards(): lax.all_to_all(cot_rows, 'seq', split_axis=2, concat_axis=1, tiled=True)  8.48 us
    all_to_all x1, waiting for transfers between devices, shards(): lax.all_to_all(back_rows(spectrum_grad), 'seq', split_axis=1, concat_axis...  7.64 us
    all_to_all x1, starting transfers between devices, shards(): lax.all_to_all(cot_rows, 'seq', split_axis=2, concat_axis=1, tiled=True)  7.11 us
  transfers between devices with their start and end apart: 5, of which 4 were waited for; matrix products, arithmetic and copies ran while one was open for 16% of the time, Pallas kernels for 0%

commit v1 on v0

--- a/solution.py
+++ b/solution.py
@@ -1,8 +1,13 @@
+import functools
 import math
 
 import jax
 import jax.numpy as jnp
+import ml_dtypes
+import numpy as np
 from jax import lax
+from jax.experimental import pallas as pl
+from jax.experimental.pallas import tpu as pltpu
 from jax.sharding import PartitionSpec as P
 
 BLOCKS = 8
@@ -90,7 +95,7 @@
     return (spectrum_grad, (in_weight_part, in_bias_part, out_weight_part, out_bias_part))
 
 
-def shards(tokens, cotangent, in_weight, in_bias, out_weight, out_bias):
+def shards_plain(tokens, cotangent, in_weight, in_bias, out_weight, out_bias):
     samples, row_count, grid_width, channels = tokens.shape
     length = row_count * lax.axis_size("seq")
     column_forward, column_inverse = column_tables(grid_width, MODES)
@@ -150,6 +155,445 @@
     )
 
 
+GROUP = math.lcm(BLOCK, 128)
+PER_GROUP = GROUP // BLOCK
+COPY_A, COPY_B, COPY_C, COPY_D, COPY_E, COPY_F = range(6)
+MESH_ID = pl.DeviceIdType.MESH
+
+
+def host_tables(length, modes):
+    residue = np.arange(length)[:, None] * np.arange(modes)[None, :] % length
+    angles = residue.astype(np.float32) * np.float32(2.0 * math.pi / length)
+    factor = np.float32(1.0 / math.sqrt(length))
+    rounded = [(f(angles) * factor).astype(ml_dtypes.bfloat16) for f in (np.cos, np.sin)]
+    return [table.astype(np.float32) for table in rounded]
+
+
+def kernel_tables(width, length, n, samples, rows):
+    local = MODES // n
+    cosine, sine = host_tables(width, MODES)
+    forward = np.stack([cosine.T, -sine.T], axis=1)
+    doubled = forward * np.where(np.arange(MODES) == 0, 1.0, 2.0)[:, None, None]
+    padded = -(-width // 16) * 16
+
+    def inverse(table):
+        table = table.reshape(n, local, 2, width)
+        whole = np.zeros((samples, padded, n, samples, local, 2), np.float32)
+        for s in range(samples):
+            whole[s, :width, :, s] = table.transpose(3, 0, 1, 2)
+        return whole.reshape(samples * padded, n * samples * local * 2)
+
+    cosine, sine = host_tables(length, length)
+    upper = np.stack([cosine, sine], axis=2)
+    lower = np.stack([-sine, cosine], axis=2)
+    turn = np.stack([upper, lower], axis=0)
+    both = samples * local
+    mixing = np.zeros((2, both, length, length, both, 2), np.float32)
+    for x in range(both):
+        mixing[:, x, :, :, x, :] = turn
+    mixing = mixing.reshape(2 * both * length, length * both * 2)
+
+    per = 4 * BLOCK // (2 * n)
+    picks = np.zeros((2, n, 16, 4 * BLOCK + 16), np.float32)
+    for r in range(2):
+        for p in range(n):
+            for i in range(16):
+                column = (r * n + p) * per + i if i < per else 4 * BLOCK + i - per
+                if i < per + 4:
+                    picks[r, p, i, column] = 1.0
+    flat = [
+        forward.reshape(2 * MODES, width),
+        doubled.reshape(2 * MODES, width),
+        inverse(doubled),
+        inverse(forward),
+        mixing,
+        mixing.T,
+        picks.reshape(2 * n * 16, 4 * BLOCK + 16),
+    ]
+    return [np.ascontiguousarray(t).astype(ml_dtypes.bfloat16) for t in flat]
+
+
+def dot(a, b, contract=(1, 0)):
+    return lax.dot_general(
+        a, b, (((contract[0],), (contract[1],)), ((), ())), preferred_element_type=jnp.float32
+    )
+
+
+def mixer(
+    n,
+    divisor,
+    tok,
+    cot,
+    col_tok,
+    col_cot,
+    inv_mix,
+    inv_grad,
+    turn,
+    turn_back,
+    picks,
+    in_weight,
+    in_bias,
+    out_weight,
+    out_bias,
+    mixed,
+    grad,
+    weight_out,
+    bias_out,
+    send_a,
+    send_b,
+    send_c,
+    send_d,
+    send_e,
+    recv_a,
+    recv_b,
+    recv_c,
+    recv_d,
+    recv_e,
+    wide,
+    spec,
+    hid,
+    slope,
+    inc,
+    pre,
+    mixed_modes,
+    grads,
+    halves,
+    half_in,
+    part,
+    gathered,
+    other,
+    send_sem,
+    recv_sem,
+    pair_send,
+    pair_recv,
+):
+    me = lax.axis_index("seq")
+    core = lax.axis_index("rep")
+    partner = 1 - core
+    samples, rows, width, channels = tok.shape
+    groups = channels // GROUP
+    padded = inv_mix.shape[0] // samples
+    chunk = send_a.shape[1]
+    row_chunk = chunk // rows
+    bf16 = jnp.bfloat16
+
+    barrier = pltpu.get_barrier_semaphore()
+
+    def greet(j, carry):
+        peer = lax.rem(me + j, n)
+        pl.semaphore_signal(barrier, inc=1, device_id={"seq": peer}, device_id_type=MESH_ID)
+        return carry
+
+    lax.fori_loop(1, n, greet, 0)
+    pl.semaphore_signal(barrier, inc=1, device_id={"rep": partner}, device_id_type=MESH_ID)
+
+    def to_peer(phase, source, target, j):
+        peer = lax.rem(me + j, n)
+        return pltpu.make_async_remote_copy(
+            src_ref=source(peer),
+            dst_ref=target.at[me],
+            send_sem=send_sem.at[phase, peer],
+            recv_sem=recv_sem.at[phase, me],
+            device_id={"seq": peer},
+            device_id_type=MESH_ID,
+        )
+
+    def from_peer(phase, target, j):
+        peer = lax.rem(me + j, n)
+        return pltpu.make_async_remote_copy(
+            src_ref=target.at[peer],
+            dst_ref=target.at[peer],
+            send_sem=send_sem.at[phase, peer],
+            recv_sem=recv_sem.at[phase, peer],
+            device_id={"seq": peer},
+            device_id_type=MESH_ID,
+        )
+
+    def each(act):
+        def step(j, carry):
+            act(j)
+            return carry
+
+        lax.fori_loop(1, n, step, 0)
+
+    def start(phase, source, target):
+        each(lambda j: to_peer(phase, lambda peer: source.at[peer], target, j).start())
+
+    def arrive(phase, target):
+        each(lambda j: from_peer(phase, target, j).wait_recv())
+
+    def drain(phase, source, target):
+        each(lambda j: to_peer(phase, lambda peer: source.at[peer], target, j).wait_send())
+
+    def columns(tokens, table, send):
+        for h in range(rows):
+            parts = [
+                dot(table[...], tokens[s, h]).reshape(n, row_chunk // samples, channels)
+                for s in range(samples)
+            ]
+            send[:, h * row_chunk : (h + 1) * row_chunk, :] = jnp.concatenate(
+                parts, axis=1
+            ).astype(bf16)
+
+    columns(tok, col_tok, send_a)
+    pl.semaphore_wait(barrier, n)
+    start(COPY_A, send_a, recv_a)
+    columns(cot, col_cot, send_b)
+    start(COPY_B, send_b, recv_b)
+    recv_a[me] = send_a[me]
+    recv_b[me] = send_b[me]
+
+    row_at = lax.broadcasted_iota(jnp.int32, (BLOCK, GROUP), 0)
+    lane_at = lax.broadcasted_iota(jnp.int32, (BLOCK, GROUP), 1)
+    for at, weight in enumerate((in_weight, out_weight)):
+        for i in range(PER_GROUP):
+            place = (lane_at == row_at + i * BLOCK).astype(bf16)
+            for c in range(2):
+                for g in range(groups):
+                    wide[2 * at + c, g, i * BLOCK : (i + 1) * BLOCK, :] = dot(
+                        weight[c, g * PER_GROUP + i], place
+                    ).astype(bf16)
+
+    half = turn.shape[0] // 2
+    scale = math.sqrt(2.0 / math.pi)
+
+    def lanes(g):
+        return pl.ds(pl.multiple_of(g * GROUP, GROUP), GROUP)
+
+    def per_group(act):
+        def step(g, carry):
+            act(g, lanes(g))
+            return carry
+
+        lax.fori_loop(0, groups, step, 0)
+
+    def along_rows(recv, at, keep, g):
+        keep[g] = dot(turn[...], recv[:, :, at].reshape(turn.shape[1], GROUP)).astype(bf16)
+
+    def back_rows(send, at):
+        send[:, :, at] = (
+            dot(turn_back[...], mixed_modes[...]).astype(bf16).reshape(n, chunk, GROUP)
+        )
+
+    def forward_group(g, at):
+        along_rows(recv_a, at, spec, g)
+        re, im = spec[g, :half], spec[g, half:]
+        w_re, w_im = wide[0, g], wide[1, g]
+        for c in range(2):
+            if c == 0:
+                value = dot(re, w_re) - dot(im, w_im)
+            else:
+                value = dot(re, w_im) + dot(im, w_re)
+            value = value + in_bias[c : c + 1, at]
+            square = value * value
+            tanh = jnp.tanh(scale * value * (1.0 + 0.044715 * square))
+            hid[g, c * half : (c + 1) * half] = (0.5 * value * (1.0 + tanh)).astype(bf16)
+            slope[g, c * half : (c + 1) * half] = 0.5 * (1.0 + tanh) + 0.5 * value * (
+                1.0 - tanh * tanh
+            ) * (scale * (1.0 + (3.0 * 0.044715) * square))
+        re, im = hid[g, :half], hid[g, half:]
+        w_re, w_im = wide[2, g], wide[3, g]
+        mixed_modes[:half] = (
+            dot(re, w_re) - dot(im, w_im) + out_bias[0:1, at]
+        ).astype(bf16)
+        mixed_modes[half:] = (
+            dot(re, w_im) + dot(im, w_re) + out_bias[1:2, at]
+        ).astype(bf16)
+        back_rows(send_c, at)
+
+    arrive(COPY_A, recv_a)
+    per_group(forward_group)
+    start(COPY_C, send_c, recv_c)
+    recv_c[me] = send_c[me]
+
+    def backward_group(g, at):
+        along_rows(recv_b, at, inc, g)
+        re, im = inc[g, :half], inc[g, half:]
+        w_re, w_im = wide[2, g], wide[3, g]
+        pre[g, :half] = (
+            (dot(re, w_re, (1, 1)) + dot(im, w_im, (1, 1))) * slope[g, :half]
+        ).astype(bf16)
+        pre[g, half:] = (
+            (dot(im, w_re, (1, 1)) - dot(re, w_im, (1, 1))) * slope[g, half:]
+        ).astype(bf16)
+        re, im = pre[g, :half], pre[g, half:]
+        w_re, w_im = wide[0, g], wide[1, g]
+        mixed_modes[:half] = (dot(re, w_re, (1, 1)) + dot(im, w_im, (1, 1))).astype(bf16)
+        mixed_modes[half:] = (dot(im, w_re, (1, 1)) - dot(re, w_im, (1, 1))).astype(bf16)
+        back_rows(send_d, at)
+
+    arrive(COPY_B, recv_b)
+    per_group(backward_group)
+    start(COPY_D, send_d, recv_d)
+    recv_d[me] = send_d[me]
+
+    def fold(product):
+        total = jnp.zeros((BLOCK, GROUP), jnp.float32)
+        for i in range(PER_GROUP):
+            inside = (lane_at >= i * BLOCK) & (lane_at < (i + 1) * BLOCK)
+            total = jnp.where(inside, product[i * BLOCK : (i + 1) * BLOCK], total)
+        return total.astype(bf16)
+
+    bias_at = lax.broadcasted_iota(jnp.int32, (16, GROUP), 0)
+
+    def grads_group(g, at):
+        bias = jnp.zeros((16, GROUP), jnp.float32)
+        for k, (left, right) in enumerate(((spec, pre), (hid, inc))):
+            a_re, a_im = left[g, :half], left[g, half:]
+            b_re, b_im = right[g, :half], right[g, half:]
+            first = 2 * k * BLOCK
+            grads[first : first + BLOCK, at] = fold(
+                dot(a_re, b_re, (0, 0)) + dot(a_im, b_im, (0, 0))
+            )
+            grads[first + BLOCK : first + 2 * BLOCK, at] = fold(
+                dot(a_re, b_im, (0, 0)) - dot(a_im, b_re, (0, 0))
+            )
+            for c, value in enumerate((b_re, b_im)):
+                total = jnp.sum(value.astype(jnp.float32), axis=0, keepdims=True)
+                bias = jnp.where(bias_at == 2 * k + c, total, bias)
+        grads[4 * BLOCK : 4 * BLOCK + 16, at] = bias.astype(bf16)
+
+    per_group(grads_group)
+    halves[...] = dot(picks[...], grads[...]).astype(bf16).reshape(halves.shape)
+
+    def swap(slot, source, target):
+        return pltpu.make_async_remote_copy(
+            src_ref=source,
+            dst_ref=target,
+            send_sem=pair_send.at[slot],
+            recv_sem=pair_recv.at[slot],
+            device_id={"rep": partner},
+            device_id_type=MESH_ID,
+        )
+
+    first_swap = swap(0, halves.at[partner], half_in)
+    first_swap.start()
+
+    def inverse(tokens, table, recv, out):
+        for h in range(rows):
+            section = recv[:, h * row_chunk : (h + 1) * row_chunk, :]
+            product = dot(table[...], section.reshape(n * row_chunk, channels))
+            for s in range(samples):
+                out[s, h] = (
+                    tokens[s, h].astype(jnp.float32)
+                    + product[s * padded : s * padded + width]
+                ).astype(bf16)
+
+    first_swap.wait()
+    send_e[...] = (
+        halves[core].astype(jnp.float32) + half_in[...].astype(jnp.float32)
+    ).astype(bf16)
+    start(COPY_E, send_e, recv_e)
+    recv_e[me] = send_e[me]
+    arrive(COPY_C, recv_c)
+    inverse(tok, inv_mix, recv_c, mixed)
+
+    arrive(COPY_E, recv_e)
+    total = jnp.sum(recv_e[...].astype(jnp.float32), axis=0) * (1.0 / divisor)
+    bias_out[...] = total
+    part[...] = total.astype(bf16)
+    each(lambda j: to_peer(COPY_F, lambda peer: part, gathered, j).start())
+    gathered[me] = part[...]
+    arrive(COPY_D, recv_d)
+    inverse(cot, inv_grad, recv_d, grad)
+    arrive(COPY_F, gathered)
+    last_swap = swap(1, gathered, other)
+    last_swap.start()
+    weight_out[core] = gathered[...]
+    last_swap.wait()
+    weight_out[partner] = other[...]
+
+    for phase, source, target in (
+        (COPY_A, send_a, recv_a),
+        (COPY_B, send_b, recv_b),
+        (COPY_C, send_c, recv_c),
+        (COPY_D, send_d, recv_d),
+        (COPY_E, send_e, recv_e),
+    ):
+        drain(phase, source, target)
+    each(lambda j: to_peer(COPY_F, lambda peer: part, gathered, j).wait_send())
+
+
+def fits(n, reps, samples, rows, channels):
+    per_row = samples * (MODES // n) * 2
+    return (
+        reps == 2
+        and MODES % n == 0
+        and per_row % 16 == 0
+        and channels % GROUP == 0
+        and channels == BLOCKS * BLOCK
+        and (4 * BLOCK) % (2 * n) == 0
+        and 4 * BLOCK // (2 * n) + 4 <= 16
+        and (samples * MODES // n * rows * n) % 16 == 0
+    )
+
+
+def shards(tokens, cotangent, in_weight, in_bias, out_weight, out_bias):
+    samples, rows, width, channels = tokens.shape
+    n, reps = lax.axis_size("seq"), lax.axis_size("rep")
+    if not fits(n, reps, samples, rows, channels):
+        return shards_plain(tokens, cotangent, in_weight, in_bias, out_weight, out_bias)
+    length = rows * n
+    chunk = rows * samples * (MODES // n) * 2
+    whole = n * chunk
+    groups = channels // GROUP
+    per = 4 * BLOCK // (2 * n)
+    tables = [jnp.asarray(t) for t in kernel_tables(width, length, n, samples, rows)]
+    bf16, f32 = jnp.bfloat16, jnp.float32
+    block = pltpu.VMEM((n, chunk, channels), bf16)
+    small = pltpu.VMEM((n, 16, channels), bf16)
+    kept = pltpu.VMEM((groups, whole, GROUP), bf16)
+    vmem = pl.BlockSpec(memory_space=pltpu.VMEM)
+    mixed, grad, weight_grad, bias_grad = pl.pallas_call(
+        functools.partial(mixer, n, float(samples * reps)),
+        out_shape=(
+            jax.ShapeDtypeStruct(tokens.shape, bf16),
+            jax.ShapeDtypeStruct(tokens.shape, bf16),
+            jax.ShapeDtypeStruct((2, n, 16, channels), bf16),
+            jax.ShapeDtypeStruct((16, channels), f32),
+        ),
+        in_specs=[vmem] * 13,
+        out_specs=(vmem,) * 4,
+        scratch_shapes=[block] * 4
+        + [small]
+        + [block] * 4
+        + [small]
+        + [
+            pltpu.VMEM((4, groups, GROUP, GROUP), bf16),
+            kept,
+            kept,
+            pltpu.VMEM((groups, whole, GROUP), f32),
+            kept,
+            kept,
+            pltpu.VMEM((whole, GROUP), bf16),
+            pltpu.VMEM((4 * BLOCK + 16, channels), bf16),
+            pltpu.VMEM((2, n, 16, channels), bf16),
+            small,
+            pltpu.VMEM((16, channels), bf16),
+            small,
+            small,
+            pltpu.SemaphoreType.DMA((6, n)),
+            pltpu.SemaphoreType.DMA((6, n)),
+            pltpu.SemaphoreType.DMA((2,)),
+            pltpu.SemaphoreType.DMA((2,)),
+        ],
+        compiler_params=pltpu.CompilerParams(
+            collective_id=0, has_side_effects=True, vmem_limit_bytes=63 << 20
+        ),
+        name="mixer",
+    )(tokens, cotangent, *tables, in_weight, in_bias, out_weight, out_bias)
+    weights = weight_grad[:, :, :per].reshape(2, 2, BLOCK, BLOCKS, BLOCK)
+    weights = weights.transpose(0, 1, 3, 2, 4).astype(f32)
+    return (
+        mixed,
+        grad,
+        weights[0],
+        bias_grad[per : per + 2],
+        weights[1],
+        bias_grad[per + 2 : per + 4],
+    )
+
+
 def solution(mesh):
     in_specs = (P("rep", "seq", None, None), P("rep", "seq", None, None), P(), P(), P(), P())
     out_specs = (P("rep", "seq", None, None), P("rep", "seq", None, None), P(), P(), P(), P())

time: 319 us -> 155 us (0.49)
  Pallas kernels: 0 us -> 135 us
  waiting for transfers between devices: 126 us -> 0 us
  blocking collectives: 49.6 us -> 0 us
  local copies, waits for them, and re-layouts: 60.8 us -> 16.6 us
  starting transfers between devices: 29.5 us -> 0 us
  matrix products: 23.1 us -> 0 us
  between operations: 14.4 us -> 0.7 us
  other arithmetic: 10.7 us -> 0.18 us
    pallas_call x0 -> x1, Pallas kernels: none -> 135 us  [shards(): pl.pallas_call(functools.partial(mixer, n, float(samples * reps)), out_sh...]
    psum x1 -> x0, waiting for transfers between devices: 88.5 us -> none  [shards(): lax.psum((partials[0], partials[1], partials[2], partials[3]), ('seq', 'r...]
    psum x1 -> x0, blocking collectives: 49.6 us -> none  [shards(): lax.psum((partials[0], partials[1], partials[2], partials[3]), ('seq', 'r...]
    all_to_all x4 -> x0, waiting for transfers between devices: 37.9 us -> none  [the longest x1 21.8 us: shards(): lax.all_to_all(spec_rows, 'seq', split_axis=2, concat_axis=1, tiled=True)]
    all_to_all x4 -> x0, starting transfers between devices: 29.5 us -> none  [the longest x1 8.72 us: shards(): lax.all_to_all(back_rows(spectrum_grad), 'seq', split_axis=1, concat_axis...]
    dot_general x14 -> x0, matrix products: 23.1 us -> none  [the longest x1 4.46 us: mix_forward(): jnp.einsum('mcbi,bciej->mebj', hidden, weights_out, preferred_element_typ...]
    reshape x5 -> x0, local copies, waits for them, and re-layouts: 17.6 us -> none  [the longest x1 4.65 us: mix_backward(): spectrum_grad = spectrum_grad.astype(jnp.bfloat16).reshape(incoming.shape)]
    convert_element_type x8 -> x2, local copies, waits for them, and re-layouts: 18 us -> 2.17 us  [shards(): weights = weights.transpose(0, 1, 3, 2, 4).astype(f32)]
  transfers between devices with their start and end apart: 5 -> 0, of which waited for: 4 -> 0; matrix products, arithmetic and copies ran while one was open for 16% -> 0% of each run, Pallas kernels for 0% -> 0%
where the time goes in v1:
time: 155 us; the launch traced here: 153 us
  Pallas kernels  135 us (87%)
  local copies, waits for them, and re-layouts  16.6 us (11%)
    pallas_call x1, Pallas kernels, shards(): pl.pallas_call(functools.partial(mixer, n, float(samples * reps)), out_sh...  135 us
    unnamed x12, local copies, waits for them, and re-layouts  12.9 us

profile of v1, /device:TPU:7, one launch (start us, length us, event | category | flops | bytes accessed | tf_op | source)
XLA Modules:
  0.0 152.8 jit_solution(14292782472344383217)
XLA Ops:
  0.6 0.0 copy-start.1
  0.6 3.0 %copy.31.tok = bf16[2,3,180,768]{3,2,1,0:T(8,128)(2,1)} copy(bf16[2,3,180,768]{3,0,2,1:T(2,128)(2,1)} %param.13) | data formatting | bytes 3317760 | tf_op args[0]
  3.6 0.0 copy-done.1
  3.6 1.4 copy.32.cot
  5.0 135.4 %mixer.1 = (bf16[2,3,180,768]{3,2,1,0:T(8,128)(2,1)}, bf16[2,3,180,768]{3,2,1,0:T(8,128)(2,1)}, bf16[2,16,16,768]{3,2,1,0:T(8,128)(2,1)}, f32[16,768]{1,0:T(8,128)}) custom-call(bf16[2,3,180,768]{3,2,1,0:T(8,128)(2,1)} %copy.31.tok, bf16[2,3,180,768]{3,2,1,0:T(8,128)(2,1)} %copy.32.cot, bf16[128,180]{1,0:T(8,128)(2,1)} %constant.14.clone.col_tok, ...), custom_call_target="tpu_custom_call" | custom-call | tf_op jit(solution)/shard_map/mixer/pallas_call | solution.py:547
  140.4 0.0 copy-start.2
  140.4 4.0 %copy.34 = bf16[2,3,180,768]{3,0,2,1:T(2,128)(2,1)} copy(bf16[2,3,180,768]{3,2,1,0:T(8,128)(2,1)} %get-tuple-element.26) | data formatting | bytes 3317760
  144.4 1.4 fusion
  145.8 0.0 copy-done.2
  145.8 0.2 slice_convert_fusion
  146.0 0.9 copy.33
  146.9 1.3 reshape.15
  148.2 0.1 slice_bitcast_fusion
  148.3 0.0 copy-start
  148.3 1.0 copy.37
  149.4 1.0 copy.36
  150.4 0.0 copy-done
  150.4 2.4 %copy.35 = bf16[2,3,180,768]{3,0,2,1:T(2,128)(2,1)} copy(bf16[2,3,180,768]{3,2,1,0:T(8,128)(2,1)S(1)} %copy-done) | data formatting | bytes 3317760
Async XLA Ops:
  0.6 3.0 %copy-start.1 = (bf16[2,3,180,768]{3,0,2,1:T(2,128)(2,1)S(1)}, bf16[2,3,180,768]{3,0,2,1:T(2,128)(2,1)}, u32[]{:S(2)}) copy-start(bf16[2,3,180,768]{3,0,2,1:T(2,128)(2,1)} %param.14) | copy-start | bytes 4976644
  140.4 5.4 %copy-start.2 = (bf16[2,16,16,768]{3,2,1,0:T(8,128)(2,1)S(1)}, bf16[2,16,16,768]{3,2,1,0:T(8,128)(2,1)}, u32[]{:S(2)}) copy-start(bf16[2,16,16,768]{3,2,1,0:T(8,128)(2,1)} %get-tuple-element.12) | copy-start | bytes 2359300
  148.3 2.1 %copy-start = (bf16[2,3,180,768]{3,2,1,0:T(8,128)(2,1)S(1)}, bf16[2,3,180,768]{3,2,1,0:T(8,128)(2,1)}, u32[]{:S(2)}) copy-start(bf16[2,3,180,768]{3,2,1,0:T(8,128)(2,1)} %get-tuple-element.27) | copy-start | bytes 4976644

commit v2 on v1

--- a/solution.py
+++ b/solution.py
@@ -157,7 +157,7 @@
 
 GROUP = math.lcm(BLOCK, 128)
 PER_GROUP = GROUP // BLOCK
-COPY_A, COPY_B, COPY_C, COPY_D, COPY_E, COPY_F = range(6)
+COPY_A, COPY_B, COPY_C, COPY_E, COPY_F, COPY_G, COPY_H, COPY_D = range(8)
 MESH_ID = pl.DeviceIdType.MESH
 
 
@@ -174,14 +174,13 @@
     cosine, sine = host_tables(width, MODES)
     forward = np.stack([cosine.T, -sine.T], axis=1)
     doubled = forward * np.where(np.arange(MODES) == 0, 1.0, 2.0)[:, None, None]
-    padded = -(-width // 16) * 16
-
-    def inverse(table):
+
+    def spread(table):
         table = table.reshape(n, local, 2, width)
-        whole = np.zeros((samples, padded, n, samples, local, 2), np.float32)
+        whole = np.zeros((n, samples, local, 2, width, samples), np.float32)
         for s in range(samples):
-            whole[s, :width, :, s] = table.transpose(3, 0, 1, 2)
-        return whole.reshape(samples * padded, n * samples * local * 2)
+            whole[:, s, :, :, :, s] = table
+        return whole.reshape(n * samples * local * 2, width * samples)
 
     cosine, sine = host_tables(length, length)
     upper = np.stack([cosine, sine], axis=2)
@@ -193,22 +192,12 @@
         mixing[:, x, :, :, x, :] = turn
     mixing = mixing.reshape(2 * both * length, length * both * 2)
 
-    per = 4 * BLOCK // (2 * n)
-    picks = np.zeros((2, n, 16, 4 * BLOCK + 16), np.float32)
-    for r in range(2):
-        for p in range(n):
-            for i in range(16):
-                column = (r * n + p) * per + i if i < per else 4 * BLOCK + i - per
-                if i < per + 4:
-                    picks[r, p, i, column] = 1.0
     flat = [
-        forward.reshape(2 * MODES, width),
-        doubled.reshape(2 * MODES, width),
-        inverse(doubled),
-        inverse(forward),
+        spread(forward),
+        spread(doubled),
+        spread(doubled).T,
+        spread(forward).T,
         mixing,
-        mixing.T,
-        picks.reshape(2 * n * 16, 4 * BLOCK + 16),
     ]
     return [np.ascontiguousarray(t).astype(ml_dtypes.bfloat16) for t in flat]
 
@@ -221,6 +210,7 @@
 
 def mixer(
     n,
+    inner,
     divisor,
     tok,
     cot,
@@ -229,8 +219,6 @@
     inv_mix,
     inv_grad,
     turn,
-    turn_back,
-    picks,
     in_weight,
     in_bias,
     out_weight,
@@ -244,11 +232,14 @@
     send_c,
     send_d,
     send_e,
+    send_f,
     recv_a,
     recv_b,
     recv_c,
     recv_d,
     recv_e,
+    recv_f,
+    turn_back,
     wide,
     spec,
     hid,
@@ -270,9 +261,10 @@
     me = lax.axis_index("seq")
     core = lax.axis_index("rep")
     partner = 1 - core
-    samples, rows, width, channels = tok.shape
+    rows, width, samples, channels = tok.shape
     groups = channels // GROUP
-    padded = inv_mix.shape[0] // samples
+    outer = n // inner
+    across, within = me // inner, lax.rem(me, inner)
     chunk = send_a.shape[1]
     row_chunk = chunk // rows
     bf16 = jnp.bfloat16
@@ -287,62 +279,111 @@
     lax.fori_loop(1, n, greet, 0)
     pl.semaphore_signal(barrier, inc=1, device_id={"rep": partner}, device_id_type=MESH_ID)
 
-    def to_peer(phase, source, target, j):
-        peer = lax.rem(me + j, n)
+    def copy_to(phase, peer, mine, source, target):
         return pltpu.make_async_remote_copy(
-            src_ref=source(peer),
-            dst_ref=target.at[me],
+            src_ref=source,
+            dst_ref=target,
             send_sem=send_sem.at[phase, peer],
-            recv_sem=recv_sem.at[phase, me],
+            recv_sem=recv_sem.at[phase, mine],
             device_id={"seq": peer},
             device_id_type=MESH_ID,
         )
 
-    def from_peer(phase, target, j):
-        peer = lax.rem(me + j, n)
-        return pltpu.make_async_remote_copy(
-            src_ref=target.at[peer],
-            dst_ref=target.at[peer],
-            send_sem=send_sem.at[phase, peer],
-            recv_sem=recv_sem.at[phase, peer],
-            device_id={"seq": peer},
-            device_id_type=MESH_ID,
-        )
-
-    def each(act):
+    def loop(count, act):
         def step(j, carry):
             act(j)
             return carry
 
-        lax.fori_loop(1, n, step, 0)
-
-    def start(phase, source, target):
-        each(lambda j: to_peer(phase, lambda peer: source.at[peer], target, j).start())
-
-    def arrive(phase, target):
-        each(lambda j: from_peer(phase, target, j).wait_recv())
-
-    def drain(phase, source, target):
-        each(lambda j: to_peer(phase, lambda peer: source.at[peer], target, j).wait_send())
+        lax.fori_loop(1, count, step, 0)
+
+    def peer_at(j):
+        return lax.rem(me + j, n)
+
+    def plane_at(j):
+        return lax.rem(within + j, inner)
+
+    def line_at(j):
+        return lax.rem(across + j, outer)
+
+    def everyone(phase, source, target, at=None):
+        cut = (lambda ref, i: ref.at[i]) if at is None else (lambda ref, i: ref.at[i, at])
+
+        def out(j):
+            peer = peer_at(j)
+            return copy_to(phase, peer, me, cut(source, peer), cut(target, me))
+
+        def back(j):
+            peer = peer_at(j)
+            return copy_to(phase, peer, peer, cut(source, peer), cut(target, peer))
+
+        return (
+            lambda: loop(n, lambda j: out(j).start()),
+            lambda: loop(n, lambda j: back(j).wait_recv()),
+            lambda: loop(n, lambda j: out(j).wait_send()),
+        )
+
+    def plane(phase, source, target):
+        def out(j):
+            v = plane_at(j)
+            peer = across * inner + v
+            return copy_to(phase, peer, me, source(v), target(within))
+
+        def back(j):
+            v = plane_at(j)
+            peer = across * inner + v
+            return copy_to(phase, peer, peer, source(v), target(v))
+
+        return (
+            lambda: loop(inner, lambda j: out(j).start()),
+            lambda: loop(inner, lambda j: back(j).wait_recv()),
+            lambda: loop(inner, lambda j: out(j).wait_send()),
+        )
+
+    def line(phase, source, target):
+        def out(j):
+            z = line_at(j)
+            peer = z * inner + within
+            return copy_to(phase, peer, me, source(z), target(across))
+
+        def back(j):
+            z = line_at(j)
+            peer = z * inner + within
+            return copy_to(phase, peer, peer, source(z), target(z))
+
+        return (
+            lambda: loop(outer, lambda j: out(j).start()),
+            lambda: loop(outer, lambda j: back(j).wait_recv()),
+            lambda: loop(outer, lambda j: out(j).wait_send()),
+        )
+
+    move_a = everyone(COPY_A, send_a, recv_a)
+    move_b = everyone(COPY_B, send_b, recv_b)
+    move_c = everyone(COPY_C, send_c, recv_c)
+    pieces = [
+        everyone(COPY_D + h, send_d, recv_d, pl.ds(h * row_chunk, row_chunk))
+        for h in range(rows)
+    ]
+    move_e = plane(COPY_E, lambda v: send_e.at[v], lambda v: recv_e.at[v])
+    move_f = line(COPY_F, lambda z: send_f.at[z], lambda z: recv_f.at[z])
+    move_g = line(COPY_G, lambda z: part, lambda z: gathered.at[within, z])
+    move_h = plane(COPY_H, lambda v: gathered.at[within], lambda v: gathered.at[v])
 
     def columns(tokens, table, send):
         for h in range(rows):
-            parts = [
-                dot(table[...], tokens[s, h]).reshape(n, row_chunk // samples, channels)
-                for s in range(samples)
-            ]
-            send[:, h * row_chunk : (h + 1) * row_chunk, :] = jnp.concatenate(
-                parts, axis=1
-            ).astype(bf16)
+            product = dot(table[...], tokens[h].reshape(width * samples, channels))
+            send[:, h * row_chunk : (h + 1) * row_chunk, :] = product.astype(bf16).reshape(
+                n, row_chunk, channels
+            )
 
     columns(tok, col_tok, send_a)
     pl.semaphore_wait(barrier, n)
-    start(COPY_A, send_a, recv_a)
+    move_a[0]()
     columns(cot, col_cot, send_b)
-    start(COPY_B, send_b, recv_b)
+    move_b[0]()
     recv_a[me] = send_a[me]
     recv_b[me] = send_b[me]
 
+    turn_back[...] = turn[...].T
     row_at = lax.broadcasted_iota(jnp.int32, (BLOCK, GROUP), 0)
     lane_at = lax.broadcasted_iota(jnp.int32, (BLOCK, GROUP), 1)
     for at, weight in enumerate((in_weight, out_weight)):
@@ -401,9 +442,9 @@
         ).astype(bf16)
         back_rows(send_c, at)
 
-    arrive(COPY_A, recv_a)
+    move_a[1]()
     per_group(forward_group)
-    start(COPY_C, send_c, recv_c)
+    move_c[0]()
     recv_c[me] = send_c[me]
 
     def backward_group(g, at):
@@ -422,10 +463,8 @@
         mixed_modes[half:] = (dot(im, w_re, (1, 1)) - dot(re, w_im, (1, 1))).astype(bf16)
         back_rows(send_d, at)
 
-    arrive(COPY_B, recv_b)
+    move_b[1]()
     per_group(backward_group)
-    start(COPY_D, send_d, recv_d)
-    recv_d[me] = send_d[me]
 
     def fold(product):
         total = jnp.zeros((BLOCK, GROUP), jnp.float32)
@@ -454,7 +493,13 @@
         grads[4 * BLOCK : 4 * BLOCK + 16, at] = bias.astype(bf16)
 
     per_group(grads_group)
-    halves[...] = dot(picks[...], grads[...]).astype(bf16).reshape(halves.shape)
+    per = 4 * BLOCK // (2 * n)
+    to_row = lax.broadcasted_iota(jnp.int32, (2 * n * 16, 4 * BLOCK + 16), 0)
+    from_row = lax.broadcasted_iota(jnp.int32, (2 * n * 16, 4 * BLOCK + 16), 1)
+    slot = to_row % 16
+    wanted = jnp.where(slot < per, to_row // 16 * per + slot, 4 * BLOCK + slot - per)
+    picks = (wanted == from_row).astype(bf16)
+    halves[...] = dot(picks, grads[...]).astype(bf16).reshape(halves.shape)
 
     def swap(slot, source, target):
         return pltpu.make_async_remote_copy(
@@ -469,49 +514,64 @@
     first_swap = swap(0, halves.at[partner], half_in)
     first_swap.start()
 
+    def inverse_row(h, tokens, table, recv, out):
+        section = recv[:, h * row_chunk : (h + 1) * row_chunk, :]
+        product = dot(table[...], section.reshape(n * row_chunk, channels))
+        kept = tokens[h].reshape(width * samples, channels).astype(jnp.float32)
+        out[h] = (kept + product).astype(bf16).reshape(width, samples, channels)
+
     def inverse(tokens, table, recv, out):
         for h in range(rows):
-            section = recv[:, h * row_chunk : (h + 1) * row_chunk, :]
-            product = dot(table[...], section.reshape(n * row_chunk, channels))
-            for s in range(samples):
-                out[s, h] = (
-                    tokens[s, h].astype(jnp.float32)
-                    + product[s * padded : s * padded + width]
-                ).astype(bf16)
+            inverse_row(h, tokens, table, recv, out)
 
     first_swap.wait()
     send_e[...] = (
-        halves[core].astype(jnp.float32) + half_in[...].astype(jnp.float32)
-    ).astype(bf16)
-    start(COPY_E, send_e, recv_e)
-    recv_e[me] = send_e[me]
-    arrive(COPY_C, recv_c)
+        (halves[core].astype(jnp.float32) + half_in[...].astype(jnp.float32))
+        .astype(bf16)
+        .reshape(send_e.shape)
+    )
+    move_e[0]()
+    recv_e[within] = send_e[within]
+    pieces[0][0]()
+    recv_d[me] = send_d[me]
+    move_c[1]()
     inverse(tok, inv_mix, recv_c, mixed)
 
-    arrive(COPY_E, recv_e)
-    total = jnp.sum(recv_e[...].astype(jnp.float32), axis=0) * (1.0 / divisor)
+    move_e[1]()
+    send_f[...] = jnp.sum(recv_e[...].astype(jnp.float32), axis=0).astype(bf16)
+    move_f[0]()
+    recv_f[across] = send_f[across]
+    middle = max(2, rows - 1)
+    for piece in pieces[1:middle]:
+        piece[0]()
+    move_f[1]()
+    total = jnp.sum(recv_f[...].astype(jnp.float32), axis=0) * (1.0 / divisor)
     bias_out[...] = total
     part[...] = total.astype(bf16)
-    each(lambda j: to_peer(COPY_F, lambda peer: part, gathered, j).start())
-    gathered[me] = part[...]
-    arrive(COPY_D, recv_d)
-    inverse(cot, inv_grad, recv_d, grad)
-    arrive(COPY_F, gathered)
+    move_g[0]()
+    gathered[within, across] = part[...]
+    for piece in pieces[middle:]:
+        piece[0]()
+    pieces[0][1]()
+    inverse_row(0, cot, inv_grad, recv_d, grad)
+    move_g[1]()
+    move_h[0]()
+    for h in range(1, rows - 1):
+        pieces[h][1]()
+        inverse_row(h, cot, inv_grad, recv_d, grad)
+    move_h[1]()
     last_swap = swap(1, gathered, other)
     last_swap.start()
-    weight_out[core] = gathered[...]
+    flat = (n, 16, channels)
+    weight_out[core] = gathered[...].reshape(flat)
+    for h in range(max(1, rows - 1), rows):
+        pieces[h][1]()
+        inverse_row(h, cot, inv_grad, recv_d, grad)
     last_swap.wait()
-    weight_out[partner] = other[...]
-
-    for phase, source, target in (
-        (COPY_A, send_a, recv_a),
-        (COPY_B, send_b, recv_b),
-        (COPY_C, send_c, recv_c),
-        (COPY_D, send_d, recv_d),
-        (COPY_E, send_e, recv_e),
-    ):
-        drain(phase, source, target)
-    each(lambda j: to_peer(COPY_F, lambda peer: part, gathered, j).wait_send())
+    weight_out[partner] = other[...].reshape(flat)
+
+    for move in (move_a, move_b, move_c, move_e, move_f, move_g, move_h, *pieces):
+        move[2]()
 
 
 def fits(n, reps, samples, rows, channels):
@@ -523,6 +583,9 @@
         and channels % GROUP == 0
         and channels == BLOCKS * BLOCK
         and (4 * BLOCK) % (2 * n) == 0
+        and n > 1
+        and n & (n - 1) == 0
+        and rows > 1
         and 4 * BLOCK // (2 * n) + 4 <= 16
         and (samples * MODES // n * rows * n) % 16 == 0
     )
@@ -534,6 +597,8 @@
     if not fits(n, reps, samples, rows, channels):
         return shards_plain(tokens, cotangent, in_weight, in_bias, out_weight, out_bias)
     length = rows * n
+    inner = 2 ** ((n.bit_length() - 1) // 2)
+    outer = n // inner
     chunk = rows * samples * (MODES // n) * 2
     whole = n * chunk
     groups = channels // GROUP
@@ -542,23 +607,27 @@
     bf16, f32 = jnp.bfloat16, jnp.float32
     block = pltpu.VMEM((n, chunk, channels), bf16)
     small = pltpu.VMEM((n, 16, channels), bf16)
+    ringed = pltpu.VMEM((inner, outer, 16, channels), bf16)
+    lined = pltpu.VMEM((outer, 16, channels), bf16)
+    planes = (tokens.transpose(1, 2, 0, 3), cotangent.transpose(1, 2, 0, 3))
     kept = pltpu.VMEM((groups, whole, GROUP), bf16)
     vmem = pl.BlockSpec(memory_space=pltpu.VMEM)
     mixed, grad, weight_grad, bias_grad = pl.pallas_call(
-        functools.partial(mixer, n, float(samples * reps)),
+        functools.partial(mixer, n, inner, float(samples * reps)),
         out_shape=(
-            jax.ShapeDtypeStruct(tokens.shape, bf16),
-            jax.ShapeDtypeStruct(tokens.shape, bf16),
+            jax.ShapeDtypeStruct(planes[0].shape, bf16),
+            jax.ShapeDtypeStruct(planes[1].shape, bf16),
             jax.ShapeDtypeStruct((2, n, 16, channels), bf16),
             jax.ShapeDtypeStruct((16, channels), f32),
         ),
-        in_specs=[vmem] * 13,
+        in_specs=[vmem] * 11,
         out_specs=(vmem,) * 4,
         scratch_shapes=[block] * 4
-        + [small]
+        + [ringed, lined]
         + [block] * 4
-        + [small]
+        + [ringed, lined]
         + [
+            pltpu.VMEM((whole, whole), bf16),
             pltpu.VMEM((4, groups, GROUP, GROUP), bf16),
             kept,
             kept,
@@ -570,10 +639,10 @@
             pltpu.VMEM((2, n, 16, channels), bf16),
             small,
             pltpu.VMEM((16, channels), bf16),
-            small,
-            small,
-            pltpu.SemaphoreType.DMA((6, n)),
-            pltpu.SemaphoreType.DMA((6, n)),
+            ringed,
+            ringed,
+            pltpu.SemaphoreType.DMA((COPY_D + rows, n)),
+            pltpu.SemaphoreType.DMA((COPY_D + rows, n)),
             pltpu.SemaphoreType.DMA((2,)),
             pltpu.SemaphoreType.DMA((2,)),
         ],
@@ -581,12 +650,12 @@
             collective_id=0, has_side_effects=True, vmem_limit_bytes=63 << 20
         ),
         name="mixer",
-    )(tokens, cotangent, *tables, in_weight, in_bias, out_weight, out_bias)
+    )(*planes, *tables, in_weight, in_bias, out_weight, out_bias)
     weights = weight_grad[:, :, :per].reshape(2, 2, BLOCK, BLOCKS, BLOCK)
     weights = weights.transpose(0, 1, 3, 2, 4).astype(f32)
     return (
-        mixed,
-        grad,
+        mixed.transpose(2, 0, 1, 3),
+        grad.transpose(2, 0, 1, 3),
         weights[0],
         bias_grad[per : per + 2],
         weights[1],

time: 155 us -> 137 us (0.88); the launches traced: 153 us -> 137 us
  Pallas kernels: 135 us -> 126 us
  local copies, waits for them, and re-layouts: 16.6 us -> 8.97 us
    pallas_call x1, Pallas kernels: 135 us -> 126 us  [shards(): pl.pallas_call(functools.partial(mixer, n, inner, float(samples * reps)),...]
    unnamed x12 -> x8, local copies, waits for them, and re-layouts: 12.9 us -> 5.27 us
where the time goes in v2:
time: 137 us
  Pallas kernels  126 us (92%)
  local copies, waits for them, and re-layouts  8.97 us (7%)
    pallas_call x1, Pallas kernels, shards(): pl.pallas_call(functools.partial(mixer, n, inner, float(samples * reps)),...  126 us
    unnamed x8, local copies, waits for them, and re-layouts  5.27 us

profile of v2, /device:TPU:7, one launch (start us, length us, event | category | flops | bytes accessed | tf_op | source)
XLA Modules:
  0.0 136.6 jit_solution(9254904803746911315)
XLA Ops:
  0.6 125.6 %mixer.1 = (bf16[3,180,2,768]{3,2,1,0:T(2,128)(2,1)}, bf16[3,180,2,768]{3,2,1,0:T(2,128)(2,1)}, bf16[2,16,16,768]{3,2,1,0:T(8,128)(2,1)}, f32[16,768]{1,0:T(8,128)}) custom-call(bf16[3,180,2,768]{3,2,1,0:T(2,128)(2,1)} %bitcast.14, bf16[3,180,2,768]{3,2,1,0:T(2,128)(2,1)} %bitcast.15, bf16[256,360]{1,0:T(8,128)(2,1)} %constant.10.clone.col_tok, ...), custom_call_target="tpu_custom_call" | custom-call | tf_op jit(solution)/shard_map/mixer/pallas_call | solution.py:615
  126.3 1.4 %fusion = (f32[2,768]{1,0:T(2,128)}, f32[2,768]{1,0:T(2,128)}) fusion(f32[16,768]{1,0:T(8,128)} %get-tuple-element.13), kind=kLoop, calls=%fused_computation.3 | loop fusion | bytes 24576 | tf_op jit(solution)/shard_map/slice | solution.py:662
  127.7 1.3 slice_convert_fusion
  129.0 0.9 copy.21
  129.9 1.3 reshape.15
  131.2 0.1 slice_bitcast_fusion
  131.3 0.0 copy-start.1
  131.3 1.0 copy.23
  132.3 1.0 copy.22
  133.4 0.0 copy-done.1
  133.4 0.0 copy-start
  133.4 1.2 copy.26
  134.5 0.9 copy-done
  135.4 1.2 copy.27
Async XLA Ops:
  131.3 2.1 %copy-start.1 = (bf16[3,180,2,768]{3,2,1,0:T(2,128)(2,1)S(1)}, bf16[3,180,2,768]{3,2,1,0:T(2,128)(2,1)}, u32[]{:S(2)}) copy-start(bf16[3,180,2,768]{3,2,1,0:T(2,128)(2,1)} %get-tuple-element.10) | copy-start | bytes 4976644
  133.4 2.0 %copy-start = (bf16[3,180,2,768]{3,2,1,0:T(2,128)(2,1)S(1)}, bf16[3,180,2,768]{3,2,1,0:T(2,128)(2,1)}, u32[]{:S(2)}) copy-start(bf16[3,180,2,768]{3,2,1,0:T(2,128)(2,1)} %get-tuple-element.11) | copy-start | bytes 4976644

commit v3 on v2

--- a/solution.py
+++ b/solution.py
@@ -225,8 +225,10 @@
     out_bias,
     mixed,
     grad,
-    weight_out,
-    bias_out,
+    in_weight_grad,
+    in_bias_grad,
+    out_weight_grad,
+    out_bias_grad,
     send_a,
     send_b,
     send_c,
@@ -253,6 +255,7 @@
     part,
     gathered,
     other,
+    both,
     send_sem,
     recv_sem,
     pair_send,
@@ -546,7 +549,8 @@
         piece[0]()
     move_f[1]()
     total = jnp.sum(recv_f[...].astype(jnp.float32), axis=0) * (1.0 / divisor)
-    bias_out[...] = total
+    in_bias_grad[...] = total[per : per + 2]
+    out_bias_grad[...] = total[per + 2 : per + 4]
     part[...] = total.astype(bf16)
     move_g[0]()
     gathered[within, across] = part[...]
@@ -562,13 +566,23 @@
     move_h[1]()
     last_swap = swap(1, gathered, other)
     last_swap.start()
-    flat = (n, 16, channels)
-    weight_out[core] = gathered[...].reshape(flat)
+    both[core] = gathered[...].reshape(n * 16, channels)
     for h in range(max(1, rows - 1), rows):
         pieces[h][1]()
         inverse_row(h, cot, inv_grad, recv_d, grad)
     last_swap.wait()
-    weight_out[partner] = other[...].reshape(flat)
+    both[partner] = other[...].reshape(n * 16, channels)
+    to_row = lax.broadcasted_iota(jnp.int32, (2 * BLOCK, n * 16), 0)
+    from_row = lax.broadcasted_iota(jnp.int32, (2 * BLOCK, n * 16), 1)
+    order = (to_row // per * 16 + to_row % per == from_row).astype(bf16)
+    for k, out in enumerate((in_weight_grad, out_weight_grad)):
+        for g in range(groups):
+            ordered = dot(order, both[k, :, g * GROUP : (g + 1) * GROUP]).astype(bf16)
+            for i in range(PER_GROUP):
+                place = (lane_at == row_at + i * BLOCK).astype(bf16)
+                block = dot(ordered, place, (1, 1))
+                for c in range(2):
+                    out[c, g * PER_GROUP + i] = block[c * BLOCK : (c + 1) * BLOCK]
 
     for move in (move_a, move_b, move_c, move_e, move_f, move_g, move_h, *pieces):
         move[2]()
@@ -602,7 +616,6 @@
     chunk = rows * samples * (MODES // n) * 2
     whole = n * chunk
     groups = channels // GROUP
-    per = 4 * BLOCK // (2 * n)
     tables = [jnp.asarray(t) for t in kernel_tables(width, length, n, samples, rows)]
     bf16, f32 = jnp.bfloat16, jnp.float32
     block = pltpu.VMEM((n, chunk, channels), bf16)
@@ -612,16 +625,18 @@
     planes = (tokens.transpose(1, 2, 0, 3), cotangent.transpose(1, 2, 0, 3))
     kept = pltpu.VMEM((groups, whole, GROUP), bf16)
     vmem = pl.BlockSpec(memory_space=pltpu.VMEM)
-    mixed, grad, weight_grad, bias_grad = pl.pallas_call(
+    mixed, grad, *parameter_grads = pl.pallas_call(
         functools.partial(mixer, n, inner, float(samples * reps)),
         out_shape=(
             jax.ShapeDtypeStruct(planes[0].shape, bf16),
             jax.ShapeDtypeStruct(planes[1].shape, bf16),
-            jax.ShapeDtypeStruct((2, n, 16, channels), bf16),
-            jax.ShapeDtypeStruct((16, channels), f32),
+            jax.ShapeDtypeStruct(in_weight.shape, f32),
+            jax.ShapeDtypeStruct(in_bias.shape, f32),
+            jax.ShapeDtypeStruct(out_weight.shape, f32),
+            jax.ShapeDtypeStruct(out_bias.shape, f32),
         ),
         in_specs=[vmem] * 11,
-        out_specs=(vmem,) * 4,
+        out_specs=(vmem,) * 6,
         scratch_shapes=[block] * 4
         + [ringed, lined]
         + [block] * 4
@@ -641,6 +656,7 @@
             pltpu.VMEM((16, channels), bf16),
             ringed,
             ringed,
+            pltpu.VMEM((2, n * 16, channels), bf16),
             pltpu.SemaphoreType.DMA((COPY_D + rows, n)),
             pltpu.SemaphoreType.DMA((COPY_D + rows, n)),
             pltpu.SemaphoreType.DMA((2,)),
@@ -651,15 +667,10 @@
         ),
         name="mixer",
     )(*planes, *tables, in_weight, in_bias, out_weight, out_bias)
-    weights = weight_grad[:, :, :per].reshape(2, 2, BLOCK, BLOCKS, BLOCK)
-    weights = weights.transpose(0, 1, 3, 2, 4).astype(f32)
     return (
         mixed.transpose(2, 0, 1, 3),
         grad.transpose(2, 0, 1, 3),
-        weights[0],
-        bias_grad[per : per + 2],
-        weights[1],
-        bias_grad[per + 2 : per + 4],
+        *parameter_grads,
     )
 
 

time: 137 us -> 137 us (level)
    unnamed x8 -> x16, local copies, waits for them, and re-layouts: 5.27 us -> 8.48 us
    convert_element_type x2 -> x0, local copies, waits for them, and re-layouts: 2.17 us -> none  [shards(): weights = weights.transpose(0, 1, 3, 2, 4).astype(f32)]
    pallas_call x1, Pallas kernels: 126 us -> 127 us  [shards(): pl.pallas_call(functools.partial(mixer, n, inner, float(samples * reps)),...]
    slice x1 -> x0, local copies, waits for them, and re-layouts: 1.42 us -> none  [shards(): bias_grad[per + 2:per + 4]]
where the time goes in v3:
time: 137 us; the launch traced here: 136 us
  Pallas kernels  127 us (93%)
  local copies, waits for them, and re-layouts  8.48 us (6%)
    pallas_call x1, Pallas kernels, shards(): pl.pallas_call(functools.partial(mixer, n, inner, float(samples * reps)),...  127 us
    unnamed x16, local copies, waits for them, and re-layouts  8.48 us

profile of v3, /device:TPU:7, one launch (start us, length us, event | category | flops | bytes accessed | tf_op | source)
XLA Modules:
  0.0 136.4 jit_solution(18353403621919019062)
XLA Ops:
  0.6 127.2 %mixer.1 = (bf16[3,180,2,768]{3,2,1,0:T(2,128)(2,1)}, bf16[3,180,2,768]{3,2,1,0:T(2,128)(2,1)}, f32[2,8,96,96]{3,2,1,0:T(8,128)}, f32[2,768]{1,0:T(2,128)}, f32[2,8,96,96]{3,2,1,0:T(8,128)}, /*index=5*/f32[2,768]{1,0:T(2,128)}) custom-call(bf16[3,180,2,768]{3,2,1,0:T(2,128)(2,1)} %bitcast.6, bf16[3,180,2,768]{3,2,1,0:T(2,128)(2,1)} %bitcast.7, ...), custom_call_target="tpu_custom_call" | custom-call | tf_op jit(solution)/shard_map/mixer/pallas_call | solution.py:628
  127.9 0.0 copy-start
  127.9 3.9 %copy.23 = bf16[2,3,180,768]{3,0,2,1:T(2,128)(2,1)} copy(bf16[2,3,180,768]{3,0,2,1:T(2,128)(2,1)} %bitcast.5) | data formatting | bytes 3317760
  131.7 0.0 copy-done
  131.7 0.0 copy-start.2
  131.7 0.0 copy-start.4
  131.7 0.0 copy-start.1
  131.8 1.2 copy.24
  132.9 0.5 copy-done.2
  133.4 0.0 copy-start.3
  133.4 0.9 copy.25
  134.3 0.0 copy-done.4
  134.3 0.6 copy.26
  134.9 0.0 copy-done.1
  134.9 0.9 copy.27
  135.8 0.0 copy-done.3
  135.8 0.6 copy.28
Async XLA Ops:
  127.9 3.9 %copy-start = (bf16[3,180,2,768]{3,2,1,0:T(2,128)(2,1)S(1)}, bf16[3,180,2,768]{3,2,1,0:T(2,128)(2,1)}, u32[]{:S(2)}) copy-start(bf16[3,180,2,768]{3,2,1,0:T(2,128)(2,1)} %get-tuple-element.13) | copy-start | bytes 4976644
  131.7 1.7 %copy-start.2 = (f32[2,8,96,96]{3,2,1,0:T(8,128)S(1)}, f32[2,8,96,96]{3,2,1,0:T(8,128)}, u32[]{:S(2)}) copy-start(f32[2,8,96,96]{3,2,1,0:T(8,128)} %get-tuple-element.26) | copy-start | bytes 1769476
  131.7 2.5 %copy-start.4 = (f32[2,768]{1,0:T(2,128)S(1)}, f32[2,768]{1,0:T(2,128)}, u32[]{:S(2)}) copy-start(f32[2,768]{1,0:T(2,128)} %get-tuple-element.27) | copy-start | bytes 18436
  131.7 3.1 %copy-start.1 = (f32[2,8,96,96]{3,2,1,0:T(8,128)S(1)}, f32[2,8,96,96]{3,2,1,0:T(8,128)}, u32[]{:S(2)}) copy-start(f32[2,8,96,96]{3,2,1,0:T(8,128)} %get-tuple-element.28) | copy-start | bytes 1769476
  133.4 2.4 %copy-start.3 = (f32[2,768]{1,0:T(2,128)S(1)}, f32[2,768]{1,0:T(2,128)}, u32[]{:S(2)}) copy-start(f32[2,768]{1,0:T(2,128)} %get-tuple-element.29) | copy-start | bytes 18436
